TPU v7x, 32 devices: a whole 2x2x4 slice. The times are simulated.
32 devices in a mesh: seq: 8 (over z, y), head: 4 (over x, core).
Axes of the slice: x: 2, y: 2, z: 4, core: 2. Of those that a mesh axis runs over, the one named last changes fastest.
Arguments:
- head_inputs: bfloat16 [8192, 5120], P('seq', 'head'), may hold values from -6 to 6
- gate_inputs: bfloat16 [8192, 5120], P('seq', 'head'), may hold values from -6 to 6
- step_raw: bfloat16 [8192, 80], P('seq', 'head'), may hold values from -9 to 256
- decay_log: float32 [80], replicated, may hold values from -12 to 0
- state_write: bfloat16 [8192, 128], P(('seq', 'head')), may hold values from -6 to 6
- state_read: bfloat16 [8192, 128], P(('seq', 'head')), may hold values from -0.5 to 0.5
- skip_gain: float32 [80], replicated, may hold values from 0.5 to 2
- norm_gain: float32 [5120], replicated, may hold values from 0.1 to 1.9
Outputs:
- scan_output: bfloat16 [8192, 5120], P('seq', 'head')
All inputs are finite; a program needn't handle non-finite values.
Results may differ from a plain program's by a relative error of at most 0.005.
Values may be sent and summed in bfloat16 or wider, within the bound.
A program may use at most 128 MiB of HBM per device.

v0:
```python
import math

import jax
import jax.numpy as jnp
from jax import lax
from jax.sharding import PartitionSpec as P

HEADS = 80
HEAD_DIM = 64
SPAN = 256


def entering_2(part, axis, combine, identity):
    place = lax.axis_index(axis)
    gathered = jax.tree.map(lambda a: lax.all_gather(a, axis), part)
    state = jax.tree.map(lambda a, e: jnp.zeros_like(a) + jnp.asarray(e, a.dtype), part, identity)

    def one(lap, state):
        return combine(
            state, jax.tree.map(lambda a: lax.dynamic_index_in_dim(a, lap, 0, False), gathered)
        )

    return lax.fori_loop(0, place, one, state)


def combine(earlier, later):
    return (earlier[0] + later[0], jnp.exp(later[0])[:, None, None] * earlier[1] + later[1])


def intra_block(values, running, step_size, scores):
    length = running.shape[1]
    row_index = lax.broadcasted_iota(jnp.int32, (length, length), 0)
    col_index = lax.broadcasted_iota(jnp.int32, (length, length), 1)
    lower = col_index <= row_index
    by_head = jnp.moveaxis(running, 2, 1)
    weight_step = jnp.moveaxis(step_size, 2, 1)
    spread = by_head[:, :, :, None] - by_head[:, :, None, :]
    mixing = (
        jnp.where(lower, jnp.exp(jnp.where(lower, spread, 0.0)), 0.0)
        * scores[:, None]
        * weight_step[:, :, None, :]
    )
    mixing = mixing.astype(jnp.bfloat16)
    return jnp.einsum("khtu,kuhp->kthp", mixing, values, preferred_element_type=jnp.float32)


def block_pieces(values, step_raw, writes, reads, decay_rate, skip_gain):
    tokens = values.shape[0]
    heads = decay_rate.shape[0]
    width = values.shape[1] // heads
    blocks = tokens // SPAN
    group = math.gcd(heads, 4)
    groups = heads // group
    step_size = jax.nn.softplus(step_raw.astype(jnp.float32)).reshape(blocks, SPAN, heads)
    running = jnp.cumsum(-decay_rate * step_size, axis=1)
    shaped = values.reshape(blocks, SPAN, heads, width)
    write_blocks = writes.reshape(blocks, SPAN, -1)
    read_blocks = reads.reshape(blocks, SPAN, -1)
    scores = jnp.einsum(
        "ktn,kun->ktu", read_blocks, write_blocks, preferred_element_type=jnp.float32
    )

    def per_group(item):
        return intra_block(item[0], item[1], item[2], scores)

    split_values = jnp.moveaxis(shaped.reshape(blocks, SPAN, groups, group, width), 2, 0)
    split_running = jnp.moveaxis(running.reshape(blocks, SPAN, groups, group), 2, 0)
    split_step = jnp.moveaxis(step_size.reshape(blocks, SPAN, groups, group), 2, 0)
    mixed_groups = lax.map(per_group, (split_values, split_running, split_step))
    local = jnp.moveaxis(mixed_groups, 0, 2).reshape(blocks, SPAN, heads, width)
    local = local + skip_gain[:, None] * shaped.astype(jnp.float32)
    tail = jnp.exp(running[:, -1:, :] - running) * step_size
    weighted = (shaped * tail[..., None]).astype(jnp.bfloat16)
    states = jnp.einsum(
        "kuhp,kun->khpn", weighted, write_blocks, preferred_element_type=jnp.float32
    )
    return (local, running, states, running[:, -1, :], read_blocks)


def within_device(totals, states):

    def advance(carry, item):
        return (combine(carry, item), carry)

    start = (jnp.zeros_like(totals[0]), jnp.zeros_like(states[0]))
    return lax.scan(advance, start, (totals, states))


def finish_blocks(local, running, read_blocks, before, earlier_state):
    entering = (jnp.exp(before[0])[:, :, None, None] * earlier_state[None] + before[1]).astype(
        jnp.bfloat16
    )
    inter = jnp.einsum("ktn,khpn->kthp", read_blocks, entering, preferred_element_type=jnp.float32)
    ssm = local + jnp.exp(running)[..., None] * inter
    return ssm.reshape(ssm.shape[0] * ssm.shape[1], -1)


def on_device(
    head_inputs, gate_inputs, step_raw, decay_log, state_write, state_read, skip_gain, norm_gain
):
    heads = head_inputs.shape[1] // HEAD_DIM
    first = lax.axis_index("head") * heads
    decay_rate = jnp.exp(lax.dynamic_slice_in_dim(decay_log, first, heads))
    skips = lax.dynamic_slice_in_dim(skip_gain, first, heads)
    gains = lax.dynamic_slice_in_dim(norm_gain, first * HEAD_DIM, heads * HEAD_DIM)
    writes, reads = (
        lax.all_gather(state_write, "head", axis=0, tiled=True),
        lax.all_gather(state_read, "head", axis=0, tiled=True),
    )
    local, running, states, totals, read_blocks = block_pieces(
        head_inputs, step_raw, writes, reads, decay_rate, skips
    )
    last, before = within_device(totals, states)
    identity = (jnp.zeros_like(last[0]), jnp.zeros_like(last[1]))
    coming = entering_2(last, "seq", combine, identity)
    earlier_state = coming[1]
    ssm = finish_blocks(local, running, read_blocks, before, earlier_state)
    gated = ssm * jax.nn.silu(gate_inputs.astype(jnp.float32))
    squares = lax.psum(jnp.sum(gated * gated, axis=1), "head")
    factor = lax.rsqrt(squares[:, None] / (HEADS * HEAD_DIM) + 1e-05)
    return (gated * factor * gains).astype(jnp.bfloat16)


def solution(mesh):
    return jax.shard_map(
        on_device,
        mesh=mesh,
        in_specs=(
            P("seq", "head"),
            P("seq", "head"),
            P("seq", "head"),
            P(),
            P(("seq", "head"), None),
            P(("seq", "head"), None),
            P(),
            P(),
        ),
        out_specs=P("seq", "head"),
        check_vma=False,
    )
```

profile of v0, /device:TPU:25, one launch (start us, length us, event | category | flops | bytes accessed | tf_op | source)
XLA Modules:
  0.0 172.2 jit_solution(16022477194663188538)
XLA Ops:
  6.5 0.9 compare_select_fusion
  7.5 0.7 exponential_negate_fusion
  8.4 2.3 %reduce-window.6 = f32[4,20,2,128]{3,1,2,0:T(8,128)S(1)} reduce-window(f32[4,20,2,128]{3,1,2,0:T(8,128)S(1)} %copy.32, f32[]{:T(128)} %constant.54.clone.1), window={size=1x1x1x128 pad=0_0x0_0x0_0x127_0}, to_apply=%region_0.1 | reduce-window | flops 2600960 | bytes 163844 | tf_op jit(solution)/shard_map/reduce-window
  11.2 6.5 %all_gather.19 = bf16[1024,128]{1,0:T(8,128)(2,1)S(1)} all-gather(bf16[256,128]{1,0:T(8,128)(2,1)} %param.18), channel_id=1, replica_groups=mesh['seq'=8,'head'=4] {'head'}, dimensions={0}, use_global_device_ids=true | all-gather | bytes 327680 | tf_op jit(solution)/shard_map/all_gather | solution.py:107
  17.7 5.1 %copy.40 = f32[1024,1280]{0,1:T(8,128)} copy(bf16[1024,1280]{1,0:T(8,128)(2,1)} %param.14) | data formatting | bytes 7864320 | tf_op jit(solution)/shard_map/convert_element_type | solution.py:71
  22.8 7.6 %reshape.65 = f32[4,256,20,64]{1,0,3,2:T(4,128)} reshape(f32[1024,1280]{0,1:T(8,128)} %copy.40) | data formatting | bytes 10485760 | tf_op jit(solution)/shard_map/convert_element_type | solution.py:71
  31.4 3.7 %multiply_convert_fusion.7 = bf16[4,256,20,64]{1,0,3,2:T(4,128)(2,1)S(1)} fusion(f32[4,256,20,64]{1,0,3,2:T(4,128)} %reshape.65, f32[4,256,20]{1,0,2:T(4,128)S(1)} %get-tuple-element.204), kind=kLoop, calls=%fused_computation.40 | loop fusion | flops 2621440 | bytes 7946240 | tf_op jit(solution)/shard_map/convert_element_type | solution.py:73
  35.1 0.8 fusion.20
  35.9 4.4 %while.41 = (s32[]{:T(128)}, f32[20]{0:T(128)S(1)}, f32[20,64,128]{2,1,0:T(8,128)S(1)}, f32[4,20]{1,0:T(4,128)S(1)}, f32[4,20,64,128]{3,2,1,0:T(8,128)}, /*index...) while((s32[]{:T(128)}, f32[20]{0:T(128)S(1)}, ...), condition=%wide.region_5.6_spmd.clone, body=%wide.region_4.5_spmd.clone.sunk | while | flops 655403 | bytes 3277569 | solution.py:86
  36.0 0.9 bitcast_dynamic-update-slice_fusion.2
  37.1 0.9 bitcast_dynamic-update-slice_fusion.2
  38.1 0.9 bitcast_dynamic-update-slice_fusion.2
  39.3 0.9 bitcast_dynamic-update-slice_fusion.2
  40.4 0.8 copy-done
  41.2 3.1 %copy.31 = bf16[1024,1280]{0,1:T(8,128)(2,1)S(1)} copy(bf16[1024,1280]{1,0:T(8,128)(2,1)} %param.14) | data formatting | bytes 5242880 | tf_op args[0]
  44.4 3.5 %reshape_reshape.6 = bf16[4,256,5,4,64]{1,0,4,3,2:T(4,128)(2,1)} reshape(bf16[1024,1280]{0,1:T(8,128)(2,1)S(1)} %copy.31) | data formatting | bytes 5242880 | tf_op jit(solution)/shard_map/reshape;reshape | solution.py:66
  47.9 5.8 %all_gather.18 = bf16[1024,128]{1,0:T(8,128)(2,1)S(1)} all-gather(bf16[256,128]{1,0:T(8,128)(2,1)S(1)} %copy-done.8), channel_id=1, replica_groups=mesh['seq'=8,'head'=4] {'head'}, dimensions={0}, use_global_device_ids=true | all-gather | bytes 327680 | tf_op jit(solution)/shard_map/all_gather | solution.py:108
  54.0 22.3 %while.39 = (s32[]{:T(128)}, f32[5,4,256,4,64]{2,4,3,1,0:T(8,128)}, bf16[5,4,256,4,64]{2,1,4,3,0:T(4,128)(2,1)}, f32[5,4,256,4]{2,1,3,0:T(4,128)}, f32[4,256,256...) while((s32[]{:T(128)}, f32[5,4,256,4,64]{2,4,3,1,0:T(8,128)}, ...), condition=%wide.region_3.4_spmd, body=%wide.region_2.3_spmd.sunk | while | flops 140574720 | bytes 3981409 | solution.py:69
  54.8 1.2 constant_dynamic-slice_fusion.7
  56.1 2.5 %fusion.37 = f32[5,4,256,4,64]{2,4,3,1,0:T(8,128)} fusion(f32[5,4,256,4,64]{2,4,3,1,0:T(8,128)} %get-tuple-element.336, s32[]{:T(128)S(6)} %copy.79, f32[4,4,256]{2,1,0:T(4,128)S(1)} %bitcast.120, f32[4,256,256]{2,1,0:T(8,128)S(1)} %get-tuple-element.346, f32[4,4,256]{2,1,0:T(4,128)S(1)} %bitcast.121, pred[256,256]{1,0:T(8,128)(4,1)S(1)} %iota_compare_fusion.2, ...), kind=kOutput, calls=%fused_computation.9.clone.1 | convolution fusion | flops 140509184 | bytes 2736132 | tf_op jit(solution)/shard_map/while/body/eval_jaxpr/khtu,kuhp->kthp/dot_general | solution.py:44
  59.3 1.2 constant_dynamic-slice_fusion.7
  60.5 2.4 %fusion.37 = f32[5,4,256,4,64]{2,4,3,1,0:T(8,128)} fusion(f32[5,4,256,4,64]{2,4,3,1,0:T(8,128)} %get-tuple-element.336, s32[]{:T(128)S(6)} %copy.79, f32[4,4,256]{2,1,0:T(4,128)S(1)} %bitcast.120, f32[4,256,256]{2,1,0:T(8,128)S(1)} %get-tuple-element.346, f32[4,4,256]{2,1,0:T(4,128)S(1)} %bitcast.121, pred[256,256]{1,0:T(8,128)(4,1)S(1)} %iota_compare_fusion.2, ...), kind=kOutput, calls=%fused_computation.9.clone.1 | convolution fusion | flops 140509184 | bytes 2736132 | tf_op jit(solution)/shard_map/while/body/eval_jaxpr/khtu,kuhp->kthp/dot_general | solution.py:44
  63.7 1.2 constant_dynamic-slice_fusion.7
  65.0 2.4 %fusion.37 = f32[5,4,256,4,64]{2,4,3,1,0:T(8,128)} fusion(f32[5,4,256,4,64]{2,4,3,1,0:T(8,128)} %get-tuple-element.336, s32[]{:T(128)S(6)} %copy.79, f32[4,4,256]{2,1,0:T(4,128)S(1)} %bitcast.120, f32[4,256,256]{2,1,0:T(8,128)S(1)} %get-tuple-element.346, f32[4,4,256]{2,1,0:T(4,128)S(1)} %bitcast.121, pred[256,256]{1,0:T(8,128)(4,1)S(1)} %iota_compare_fusion.2, ...), kind=kOutput, calls=%fused_computation.9.clone.1 | convolution fusion | flops 140509184 | bytes 2736132 | tf_op jit(solution)/shard_map/while/body/eval_jaxpr/khtu,kuhp->kthp/dot_general | solution.py:44
  68.2 1.2 constant_dynamic-slice_fusion.7
  69.4 2.5 %fusion.37 = f32[5,4,256,4,64]{2,4,3,1,0:T(8,128)} fusion(f32[5,4,256,4,64]{2,4,3,1,0:T(8,128)} %get-tuple-element.336, s32[]{:T(128)S(6)} %copy.79, f32[4,4,256]{2,1,0:T(4,128)S(1)} %bitcast.120, f32[4,256,256]{2,1,0:T(8,128)S(1)} %get-tuple-element.346, f32[4,4,256]{2,1,0:T(4,128)S(1)} %bitcast.121, pred[256,256]{1,0:T(8,128)(4,1)S(1)} %iota_compare_fusion.2, ...), kind=kOutput, calls=%fused_computation.9.clone.1 | convolution fusion | flops 140509184 | bytes 2736132 | tf_op jit(solution)/shard_map/while/body/eval_jaxpr/khtu,kuhp->kthp/dot_general | solution.py:44
  72.7 1.2 constant_dynamic-slice_fusion.7
  73.9 2.4 %fusion.37 = f32[5,4,256,4,64]{2,4,3,1,0:T(8,128)} fusion(f32[5,4,256,4,64]{2,4,3,1,0:T(8,128)} %get-tuple-element.336, s32[]{:T(128)S(6)} %copy.79, f32[4,4,256]{2,1,0:T(4,128)S(1)} %bitcast.120, f32[4,256,256]{2,1,0:T(8,128)S(1)} %get-tuple-element.346, f32[4,4,256]{2,1,0:T(4,128)S(1)} %bitcast.121, pred[256,256]{1,0:T(8,128)(4,1)S(1)} %iota_compare_fusion.2, ...), kind=kOutput, calls=%fused_computation.9.clone.1 | convolution fusion | flops 140509184 | bytes 2736132 | tf_op jit(solution)/shard_map/while/body/eval_jaxpr/khtu,kuhp->kthp/dot_general | solution.py:44
  76.3 5.6 %copy.39 = f32[4,256,5,4,64]{1,4,3,2,0:T(8,128)} copy(f32[4,256,5,4,64]{1,4,3,0,2:T(8,128)} %bitcast.112) | data formatting | bytes 10485760 | tf_op jit(solution)/shard_map/transpose | solution.py:70
  84.6 15.6 %all-reduce = f32[160]{0:T(256)S(1)} all-reduce(f32[160]{0:T(256)S(1)} %dynamic-update-slice), channel_id=2, replica_groups=mesh['seq'=8,'head'=4] {'seq'}, use_global_device_ids=true, to_apply=%add | all-reduce | flops 160 | bytes 1280
  100.3 3.0 %copy.47 = bf16[1024,1280]{0,1:T(8,128)(2,1)S(1)} copy(bf16[1024,1280]{1,0:T(8,128)(2,1)} %param.15) | data formatting | bytes 5242880 | tf_op args[1]
  103.4 0.8 dynamic_slice.40
  104.1 22.4 %all-gather.4.cloned.1.call-done = f32[160,64,128]{2,1,0:T(8,128)} async-done(((f32[20,64,128]{2,1,0:T(8,128)}), f32[160,64,128]{2,1,0:T(8,128)}) %all-gather.4.cloned.1.call-update) | async-done | bytes 5242896 | tf_op jit(solution)/shard_map/all_gather | solution.py:15
  126.6 8.0 %while.40 = (s32[]{:T(128)}, f32[20,64,128]{2,1,0:T(8,128)S(1)}, s32[]{:T(128)}, f32[8,20]{1,0:T(8,128)S(1)}, f32[8,20,64,128]{3,2,1,0:T(8,128)}, /*index=5*/s32[]{:T(128)}, s32[]{:T(128)}, s32[]{:T(128)}) while((s32[]{:T(128)}, f32[20,64,128]{2,1,0:T(8,128)S(1)}, s32[]{:T(128)}, f32[8,20]{1,0:T(8,128)S(1)}, f32[8,20,64,128]{3,2,1,0:T(8,128)}, ...), condition=%wide.region_7.8_spmd, body=%wide.region_6.7_spmd.sunk | while | flops 327685 | bytes 1966455 | solution.py:23
  126.6 1.3 bitcast_add_fusion.4
  127.9 1.3 bitcast_add_fusion.4
  129.2 1.3 bitcast_add_fusion.4
  130.5 1.3 bitcast_add_fusion.4
  131.8 1.3 bitcast_add_fusion.4
  133.1 1.3 bitcast_add_fusion.4
  134.6 6.5 %fusion.18 = f32[4,256,20,64]{1,3,2,0:T(8,128)S(1)} fusion(f32[4,256,20,64]{1,3,2,0:T(8,128)} %bitcast.109, f32[4,256,20,64]{1,0,3,2:T(4,128)} %reshape.65, f32[4,256,20]{1,2,0:T(8,128)} %copy.42, f32[20]{0:T(128)} %dynamic_slice.39, bf16[4,256,128,1]{2,1,3,0:T(8,128)(2,1)S(1)} %bitcast.114, f32[4,20,64,128]{3,2,1,0:T(8,128)} %get-tuple-element.126, ...), kind=kOutput, calls=%fused_computation.35 | convolution fusion | flops 342753280 | bytes 19349904 | tf_op jit(solution)/shard_map/ktn,khpn->kthp/dot_general | solution.py:93
  141.1 3.9 %copy.46 = f32[4,256,20,64]{1,0,3,2:T(4,128)S(1)} copy(f32[4,256,20,64]{1,3,2,0:T(8,128)S(1)} %fusion.18) | data formatting | bytes 10485760 | tf_op jit(solution)/shard_map/add | solution.py:94
  145.0 1.3 copy.54
  146.3 2.3 %copy-done.1 = f32[160,8,4,256]{3,1,2,0:T(8,128)} copy-done((f32[160,8,4,256]{3,1,2,0:T(8,128)}, f32[160,8,4,256]{3,1,2,0:T(8,128)S(1)}, u32[]{:S(2)}) %copy-start.1) | copy-done | bytes 5242904
  148.6 1.8 %multiply_reduce_fusion = f32[1024]{0:T(1024)S(1)} fusion(f32[1024,1280]{0,1:T(8,128)S(1)} %bitcast.107, bf16[1024,1280]{0,1:T(8,128)(2,1)S(1)} %copy.47), kind=kLoop, calls=%fused_computation.39 | loop fusion | flops 10484736 | bytes 7868416 | tf_op jit(solution)/shard_map/reduce_sum | solution.py:119
  150.3 5.7 %psum.7 = f32[1024]{0:T(1024)S(1)} all-reduce(f32[1024]{0:T(1024)S(1)} %multiply_reduce_fusion), channel_id=1, replica_groups=mesh['seq'=8,'head'=4] {'head'}, use_global_device_ids=true, to_apply=%region_9.10 | all-reduce | flops 1024 | bytes 8192 | tf_op jit(solution)/shard_map/psum | solution.py:119
  156.0 5.0 %multiply_convert_fusion.6 = bf16[1024,1280]{0,1:T(8,128)(2,1)} fusion(f32[1280]{0:T(1024)S(1)} %dynamic_slice.40, f32[1024]{0:T(1024)S(1)} %add_rsqrt_fusion, f32[1024,1280]{0,1:T(8,128)} %bitcast.108, bf16[1024,1280]{0,1:T(8,128)(2,1)S(1)} %copy.47), kind=kLoop, calls=%fused_computation.38 | loop fusion | flops 11796480 | bytes 10494976 | tf_op jit(solution)/shard_map/convert_element_type | solution.py:121
  161.0 4.4 %copy.48 = bf16[1024,1280]{1,0:T(8,128)(2,1)} copy(bf16[1024,1280]{0,1:T(8,128)(2,1)} %multiply_convert_fusion.6) | data formatting | bytes 5242880 | tf_op jit(solution)/shard_map/convert_element_type | solution.py:121
  (92 shorter events, 8.9 us)
Async XLA Ops:
  6.5 120.0 %all-gather.4.cloned.1.call-start = ((), (), s32[]{:S(2)}) async-start(), calls=%async_computation | async-start | bytes 5898240 | tf_op jit(solution)/shard_map/all_gather | solution.py:15
  7.4 1.0 copy-start.5
  11.2 19.5 %copy-start.4 = (f32[4,20,256]{2,0,1:T(4,128)}, f32[4,20,256]{2,0,1:T(4,128)S(1)}, u32[]{:S(2)}) copy-start(f32[4,20,256]{2,0,1:T(4,128)S(1)} %reduce_window_sum.16) | copy-start | bytes 245764
  17.7 17.4 %copy-start.2 = (bf16[1024,128]{1,0:T(8,128)(2,1)}, bf16[1024,128]{1,0:T(8,128)(2,1)S(1)}, u32[]{:S(2)}) copy-start(bf16[1024,128]{1,0:T(8,128)(2,1)S(1)} %all_gather.19) | copy-start | bytes 786436
  40.3 0.8 copy-start
  40.3 4.0 %copy-start.6 = (f32[1024,20]{0,1:T(8,128)S(1)}, f32[1024,20]{0,1:T(8,128)}, u32[]{:S(2)}) copy-start(f32[1024,20]{0,1:T(8,128)} %copy-done.5) | copy-start | bytes 245764
  41.2 6.7 %copy-start.8 = (bf16[256,128]{1,0:T(8,128)(2,1)S(1)}, bf16[256,128]{1,0:T(8,128)(2,1)}, u32[]{:S(2)}) copy-start(bf16[256,128]{1,0:T(8,128)(2,1)} %param.19) | copy-start | bytes 196612
  41.2 12.5 %copy-start.3 = (bf16[1024,128]{1,0:T(8,128)(2,1)S(1)}, bf16[1024,128]{1,0:T(8,128)(2,1)}, u32[]{:S(2)}) copy-start(bf16[1024,128]{1,0:T(8,128)(2,1)} %copy-done.2) | copy-start | bytes 786436
  76.3 5.6 %copy-start.7 = (f32[4,256,20]{1,0,2:T(4,128)S(1)}, f32[4,256,20]{1,0,2:T(4,128)}, u32[]{:S(2)}) copy-start(f32[4,256,20]{1,0,2:T(4,128)} %get-tuple-element.205) | copy-start | bytes 245764
  76.3 6.3 %copy-start.9 = (f32[80]{0:T(128)S(1)}, f32[80]{0:T(128)}, u32[]{:S(2)}) copy-start(f32[80]{0:T(128)} %param.20) | copy-start | bytes 964
  76.3 6.8 %copy-start.10 = (u32[32]{0:T(128)S(1)}, u32[32]{0:T(128)}, u32[]{:S(2)}) copy-start(u32[32]{0:T(128)} %constant.84) | copy-start | bytes 388
  146.3 2.3 %copy-start.1 = (f32[160,8,4,256]{3,1,2,0:T(8,128)}, f32[160,8,4,256]{3,1,2,0:T(8,128)S(1)}, u32[]{:S(2)}) copy-start(f32[160,8,4,256]{3,1,2,0:T(8,128)S(1)} %copy.54) | copy-start | bytes 15728644
Sparse Core Ops, SparseCore 0:
  41.3 85.1 all-gather.3
where the time goes:
time: 175 us; the launch traced here: 172 us
  local copies, waits for them, and re-layouts  54.4 us (31%)
  blocking collectives  33.6 us (19%)
  other arithmetic  27.1 us (15%)
  waiting for transfers between devices  22.4 us (13%)
  matrix products  19.9 us (11%)
  between operations  14.3 us (8%)
    all_gather x1, waiting for transfers between devices, entering_2(): gathered = jax.tree.map(lambda a: lax.all_gather(a, axis), part)  22.4 us
    unnamed x1, blocking collectives  15.6 us
    convert_element_type x2, local copies, waits for them, and re-layouts, block_pieces(): local = local + skip_gain[:, None] * shaped.astype(jnp.float32)  12.7 us
    dot_general x5, matrix products, intra_block(): jnp.einsum('khtu,kuhp->kthp', mixing, values, preferred_element_type=jnp....  12.2 us
    unnamed x28, local copies, waits for them, and re-layouts  11.4 us
    dynamic_slice x20, local copies, waits for them, and re-layouts, block_pieces(): mixed_groups = lax.map(per_group, (split_values, split_running, split_step))  9.83 us
    add x10, other arithmetic, combine(): jnp.exp(later[0])[:, None, None] * earlier[1] + later[1]  8.03 us
    dot_general x1, matrix products, finish_blocks(): jnp.einsum('ktn,khpn->kthp', read_blocks, entering, preferred_element_typ...  6.51 us
  transfers between devices with their start and end apart: 1, of which 1 were waited for; matrix products, arithmetic and copies ran while one was open for 24% of the time, Pallas kernels for 0%

commit v1 on v0

v1 whole, which is shorter than its diff:
```python
import functools
import math

import jax
import jax.numpy as jnp
from jax import lax
from jax.experimental import pallas as pl
from jax.experimental.pallas import tpu as pltpu
from jax.sharding import PartitionSpec as P

HEAD_DIM = 64
L = 128
LOG2E = math.log2(math.e)
F32 = jnp.float32
BF16 = jnp.bfloat16
MESH = pl.DeviceIdType.MESH
CAP = 100.0


def decays(raw_ref, rate_ref, pad_a, pad_s, heads):
    raw = raw_ref[...].astype(F32)
    step = jnp.maximum(raw, 0.0) + jnp.log1p(jnp.exp(-jnp.abs(raw)))
    pad_a[...] = jnp.zeros_like(pad_a)
    pad_s[...] = jnp.zeros_like(pad_s)
    pad_a[:, :heads] = -rate_ref[...] * step
    pad_s[:, :heads] = jnp.log2(step)
    row = lax.broadcasted_iota(jnp.int32, (L, L), 0)
    col = lax.broadcasted_iota(jnp.int32, (L, L), 1)
    tri = jnp.where(col <= row, 1.0, 0.0).astype(F32)
    run = jnp.dot(
        tri, pad_a[...], preferred_element_type=F32, precision=lax.Precision.HIGHEST
    )
    return run, run - pad_s[...]


def pair_lanes(cols, j, rows):
    lane = lax.broadcasted_iota(jnp.int32, (rows, L), 1)
    first = jnp.broadcast_to(cols[:, 2 * j : 2 * j + 1], (rows, L))
    second = jnp.broadcast_to(cols[:, 2 * j + 1 : 2 * j + 2], (rows, L))
    return jnp.where(lane < HEAD_DIM, first, second)


def state_kernel(
    heads, tiles, x_ref, raw_ref, rate_ref, write_ref,
    loc_ref, pre_ref, fin_ref, tot_ref, pad_a, pad_s, carry, total,
):
    chunk = pl.program_id(0)

    @pl.when(chunk == 0)
    def _():
        carry[...] = jnp.zeros_like(carry)
        total[...] = jnp.zeros_like(total)

    run, run_u = decays(raw_ref, rate_ref, pad_a, pad_s, heads)
    last = run[L - 1 : L, :]
    tail = jnp.exp2(last - run_u)
    write_t = write_ref[...].astype(F32).T.astype(BF16)
    pre_ref[0] = total[...]
    for j in range(tiles):
        x = x_ref[:, j * L : (j + 1) * L].astype(F32)
        weighted = (pair_lanes(tail, j, L) * x).astype(BF16)
        new = jnp.dot(write_t, weighted, preferred_element_type=F32)
        gone = pair_lanes(last, j, 1)
        old = carry[j]
        loc_ref[0, j] = old.astype(BF16)
        now = jnp.exp2(gone) * old + new
        carry[j] = now
        fin_ref[j] = now.astype(BF16)
        total[j : j + 1, :] = total[j : j + 1, :] + gone
    tot_ref[...] = total[...]


def exchange_kernel(
    count, tiles, group, fin_ref, tot_ref, out_ref,
    mate_buf, mate_tot, chain_in, chain_out,
    s_mate, r_mate, s_tot, r_tot, s_chain, r_chain,
):
    me = lax.axis_index("seq")
    odd = lax.rem(me, 2)
    pairs = count // 2
    place = me // 2
    mate = me + 1 - 2 * odd
    after = lax.rem(me + 2, count)
    before = lax.rem(me + count - 2, count)
    has_before = place > 0
    has_after = place < pairs - 1

    barrier = pltpu.get_barrier_semaphore()
    for other in (mate, after, before):
        pl.semaphore_signal(barrier, inc=1, device_id={"seq": other}, device_id_type=MESH)
    pl.semaphore_wait(barrier, 3)

    pieces = tiles // group

    def to_mate(p):
        part = pl.ds(p * group, group)
        return pltpu.make_async_remote_copy(
            src_ref=fin_ref.at[part], dst_ref=mate_buf.at[part],
            send_sem=s_mate.at[p], recv_sem=r_mate.at[p],
            device_id={"seq": mate}, device_id_type=MESH,
        )

    def to_next(p):
        part = pl.ds(p * group, group)
        return pltpu.make_async_remote_copy(
            src_ref=chain_out.at[part], dst_ref=chain_in.at[part],
            send_sem=s_chain.at[p], recv_sem=r_chain.at[p],
            device_id={"seq": after}, device_id_type=MESH,
        )

    tot_copy = pltpu.make_async_remote_copy(
        src_ref=tot_ref, dst_ref=mate_tot, send_sem=s_tot, recv_sem=r_tot,
        device_id={"seq": mate}, device_id_type=MESH,
    )
    tot_copy.start()
    for p in range(pieces):
        to_mate(p).start()

    @pl.when(jnp.logical_not(has_before))
    def _():
        chain_in[...] = jnp.zeros_like(chain_in)

    tot_copy.wait_recv()
    is_odd = odd == 1
    for p in range(pieces):
        to_mate(p).wait_recv()

        @pl.when(has_before)
        def _():
            to_next(p).wait_recv()

        for j in range(p * group, (p + 1) * group):
            own_tot = jnp.exp2(tot_ref[j : j + 1, :])
            other_tot = jnp.exp2(mate_tot[j : j + 1, :])
            own = fin_ref[j].astype(F32)
            other = mate_buf[j].astype(F32)
            coming = chain_in[j].astype(F32)
            early = jnp.where(is_odd, other, own)
            late = jnp.where(is_odd, own, other)
            early_tot = jnp.where(is_odd, other_tot, own_tot)
            late_tot = jnp.where(is_odd, own_tot, other_tot)
            middle = early_tot * coming + early
            chain_out[j] = (late_tot * middle + late).astype(BF16)
            out_ref[j] = jnp.where(is_odd, middle, coming)

        @pl.when(has_after)
        def _():
            to_next(p).start()

    tot_copy.wait_send()
    for p in range(pieces):
        to_mate(p).wait_send()

        @pl.when(has_after)
        def _():
            to_next(p).wait_send()


def output_kernel(
    heads, tiles, x_ref, z_ref, raw_ref, rate_ref, write_ref, read_ref,
    loc_ref, pre_ref, coming_ref, skip_ref,
    gated_ref, square_ref, pad_a, pad_s,
):
    run, run_u = decays(raw_ref, rate_ref, pad_a, pad_s, heads)
    run_rows = run_u.T
    grown = jnp.exp2(run)
    reads = read_ref[...]
    scores = lax.dot_general(
        reads, write_ref[...], (((1,), (1,)), ((), ())), preferred_element_type=F32
    )
    row = lax.broadcasted_iota(jnp.int32, (L, L), 0)
    col = lax.broadcasted_iota(jnp.int32, (L, L), 1)
    scores = jnp.where(col <= row, scores, 0.0)
    left = col < HEAD_DIM
    squares = jnp.zeros((L, L), F32)
    for j in range(tiles):
        x = x_ref[:, j * L : (j + 1) * L]
        mixes = []
        for k in (2 * j, 2 * j + 1):
            spread = run[:, k : k + 1] - run_rows[k : k + 1, :]
            mixes.append((scores * jnp.exp2(jnp.minimum(spread, CAP))).astype(BF16))
        wide = x.astype(F32)
        top = jnp.where(left, wide, 0.0).astype(BF16)
        bottom = jnp.where(left, 0.0, wide).astype(BF16)
        local = jnp.dot(
            jnp.concatenate(mixes, axis=1), jnp.concatenate([top, bottom], axis=0),
            preferred_element_type=F32,
        )
        entering = (
            loc_ref[0, j].astype(F32) + jnp.exp2(pre_ref[0, j : j + 1, :]) * coming_ref[j]
        ).astype(BF16)
        inter = jnp.dot(reads, entering, preferred_element_type=F32)
        y = local + skip_ref[j : j + 1, :] * wide + pair_lanes(grown, j, L) * inter
        z = z_ref[:, j * L : (j + 1) * L].astype(F32)
        gated = y * z * jax.nn.sigmoid(z)
        gated_ref[:, j * L : (j + 1) * L] = gated.astype(BF16)
        squares = squares + gated * gated
    square_ref[0] = jnp.sum(squares.T, axis=0, keepdims=True)


def on_device(
    count, head_inputs, gate_inputs, step_raw, decay_log, state_write, state_read, skip_gain, norm_gain
):
    tokens, inner = head_inputs.shape
    heads = inner // HEAD_DIM
    tiles = inner // L
    chunks = tokens // L
    states = state_write.shape[1]
    first = lax.axis_index("head") * heads
    rate = (LOG2E * jnp.exp(lax.dynamic_slice_in_dim(decay_log, first, heads))).reshape(1, heads)
    skips = lax.dynamic_slice_in_dim(skip_gain, first, heads)
    skips = jnp.broadcast_to(skips[:, None], (heads, HEAD_DIM)).reshape(tiles, L)
    gains = lax.dynamic_slice_in_dim(norm_gain, first * HEAD_DIM, inner)
    maps = lax.all_gather(
        jnp.concatenate([state_write, state_read], axis=1), "head", axis=0, tiled=True
    )
    group = math.gcd(tiles, 2)
    pieces = tiles // group
    sds = jax.ShapeDtypeStruct
    whole = lambda *shape: pl.BlockSpec(shape, lambda c: (0,) * len(shape))
    wide = pl.BlockSpec((L, inner), lambda c: (c, 0))
    raw_spec = pl.BlockSpec((L, heads), lambda c: (c, 0))
    write_spec = pl.BlockSpec((L, states), lambda c: (c, 0))
    read_spec = pl.BlockSpec((L, states), lambda c: (c, 1))
    loc_spec = pl.BlockSpec((1, tiles, states, L), lambda c: (c, 0, 0, 0))
    pre_spec = pl.BlockSpec((1, tiles, L), lambda c: (c, 0, 0))
    pads = [pltpu.VMEM((L, L), F32), pltpu.VMEM((L, L), F32)]

    loc, pre, fin, tot = pl.pallas_call(
        functools.partial(state_kernel, heads, tiles),
        grid=(chunks,),
        in_specs=[wide, raw_spec, whole(1, heads), write_spec],
        out_specs=[loc_spec, pre_spec, whole(tiles, states, L), whole(tiles, L)],
        out_shape=[
            sds((chunks, tiles, states, L), BF16),
            sds((chunks, tiles, L), F32),
            sds((tiles, states, L), BF16),
            sds((tiles, L), F32),
        ],
        scratch_shapes=pads + [pltpu.VMEM((tiles, states, L), F32), pltpu.VMEM((tiles, L), F32)],
        name="states",
    )(head_inputs, step_raw, rate, maps)

    vmem = pl.BlockSpec(memory_space=pltpu.VMEM)
    buf = pltpu.VMEM((tiles, states, L), BF16)
    sems = pltpu.SemaphoreType.DMA((pieces,))
    coming = pl.pallas_call(
        functools.partial(exchange_kernel, count, tiles, group),
        in_specs=[vmem, vmem],
        out_specs=vmem,
        out_shape=sds((tiles, states, L), F32),
        scratch_shapes=[
            buf, pltpu.VMEM((tiles, L), F32), buf, buf,
            sems, sems, pltpu.SemaphoreType.DMA, pltpu.SemaphoreType.DMA, sems, sems,
        ],
        compiler_params=pltpu.CompilerParams(collective_id=0, has_side_effects=True),
        name="exchange",
    )(fin, tot)

    gated, squares = pl.pallas_call(
        functools.partial(output_kernel, heads, tiles),
        grid=(chunks,),
        in_specs=[
            wide, wide, raw_spec, whole(1, heads), write_spec, read_spec,
            loc_spec, pre_spec, whole(tiles, states, L), whole(tiles, L),
        ],
        out_specs=[wide, pl.BlockSpec((1, 1, L), lambda c: (c, 0, 0))],
        out_shape=[sds((tokens, inner), BF16), sds((chunks, 1, L), F32)],
        scratch_shapes=pads,
        name="outputs",
    )(head_inputs, gate_inputs, step_raw, rate, maps, maps, loc, pre, coming, skips)

    squares = lax.psum(squares, "head")
    factor = lax.rsqrt(squares.reshape(tokens, 1) / norm_gain.shape[0] + 1e-05)
    return (gated.astype(F32) * factor * gains).astype(BF16)


def solution(mesh):
    return jax.shard_map(
        functools.partial(on_device, mesh.shape["seq"]),
        mesh=mesh,
        in_specs=(
            P("seq", "head"),
            P("seq", "head"),
            P("seq", "head"),
            P(),
            P(("seq", "head"), None),
            P(("seq", "head"), None),
            P(),
            P(),
        ),
        out_specs=P("seq", "head"),
        check_vma=False,
    )
```

time: 175 us -> 70.4 us (0.40); the launches traced: 172 us -> 69.8 us
  local copies, waits for them, and re-layouts: 54.4 us -> 3.36 us
  Pallas kernels: 0 us -> 44.8 us
  waiting for transfers between devices: 22.4 us -> 0 us
  other arithmetic: 27.1 us -> 6.04 us
  matrix products: 19.9 us -> 0 us
  blocking collectives: 33.6 us -> 15.6 us
  between operations: 14.3 us -> 0.04 us
    pallas_call x0 -> x3, Pallas kernels: none -> 44.8 us  [the longest x1 21.4 us: on_device(): pl.pallas_call(functools.partial(exchange_kernel, count, tiles, group), i...]
    all_gather x1 -> x0, waiting for transfers between devices: 22.4 us -> none  [entering_2(): gathered = jax.tree.map(lambda a: lax.all_gather(a, axis), part)]
    dot_general x8 -> x0, matrix products: 19.9 us -> none  [the longest x5 12.2 us: intra_block(): jnp.einsum('khtu,kuhp->kthp', mixing, values, preferred_element_type=jnp....]
    convert_element_type x3 -> x0, local copies, waits for them, and re-layouts: 17.1 us -> none  [the longest x2 12.7 us: block_pieces(): local = local + skip_gain[:, None] * shaped.astype(jnp.float32)]
    unnamed x1 -> x0, blocking collectives: 15.6 us -> none
    dynamic_slice x21 -> x1, local copies, waits for them, and re-layouts: 10.6 us -> 0.79 us  [on_device(): gains = lax.dynamic_slice_in_dim(norm_gain, first * HEAD_DIM, inner)]
    unnamed x28 -> x3, local copies, waits for them, and re-layouts: 11.4 us -> 1.66 us
    add x10 -> x0, other arithmetic: 8.03 us -> none  [combine(): jnp.exp(later[0])[:, None, None] * earlier[1] + later[1]]
  transfers between devices with their start and end apart: 1 -> 0, of which waited for: 1 -> 0; matrix products, arithmetic and copies ran while one was open for 24% -> 0% of each run, Pallas kernels for 0% -> 0%
where the time goes in v1:
time: 70.4 us; the launch traced here: 69.8 us
  Pallas kernels  44.8 us (64%)
  blocking collectives  15.6 us (22%)
  other arithmetic  6.04 us (9%)
  local copies, waits for them, and re-layouts  3.36 us (5%)
    pallas_call x1, Pallas kernels, on_device(): pl.pallas_call(functools.partial(exchange_kernel, count, tiles, group), i...  21.4 us
    pallas_call x1, Pallas kernels, on_device(): pl.pallas_call(functools.partial(output_kernel, heads, tiles), grid=(chun...  13.6 us
    pallas_call x1, Pallas kernels, on_device(): pl.pallas_call(functools.partial(state_kernel, heads, tiles), grid=(chunk...  9.76 us
    all_gather x1, blocking collectives, on_device(): lax.all_gather(jnp.concatenate([state_write, state_read], axis=1), 'head'...  8.13 us
    psum x1, blocking collectives, on_device(): squares = lax.psum(squares, 'head')  7.44 us
    convert_element_type x1, other arithmetic, on_device(): return (gated.astype(F32) * factor * gains).astype(BF16)  3.89 us
    unnamed x3, local copies, waits for them, and re-layouts  1.66 us

profile of v1, /device:TPU:25, one launch (start us, length us, event | category | flops | bytes accessed | tf_op | source)
XLA Modules:
  0.0 69.8 jit_solution(1846380157358922)
XLA Ops:
  0.0 1.2 %multiply_bitcast_fusion.rate_ref = f32[1,20]{1,0:T(1,128)} fusion(f32[80]{0:T(128)} %param.11, s32[]{:T(128)S(6)} %select_n.7), kind=kLoop, calls=%fused_computation.3 | loop fusion | flops 20 | bytes 164 | tf_op jit(solution)/shard_map/reshape | solution.py:210
  1.2 0.9 %pad_maximum_fusion = bf16[256,256]{1,0:T(8,128)(2,1)S(1)} fusion(bf16[256,128]{1,0:T(8,128)(2,1)} %param.13, bf16[256,128]{1,0:T(8,128)(2,1)} %param.12), kind=kLoop, calls=%fused_computation.1 | loop fusion | flops 262144 | bytes 262144 | tf_op jit(solution)/shard_map/concatenate | solution.py:215
  2.1 0.0 copy-start
  2.1 8.1 %all_gather.3.write_ref.read_ref = bf16[1024,256]{1,0:T(8,128)(2,1)} all-gather(bf16[256,256]{1,0:T(8,128)(2,1)S(1)} %pad_maximum_fusion), channel_id=1, replica_groups=mesh['seq'=8,'head'=4] {'head'}, dimensions={0}, use_global_device_ids=true | all-gather | bytes 655360 | tf_op jit(solution)/shard_map/all_gather | solution.py:214
  10.3 1.7 %copy.12.raw_ref = bf16[1024,20]{1,0:T(8,128)(2,1)} copy(bf16[1024,20]{0,1:T(8,128)(2,1)} %param.10) | data formatting | bytes 81920 | tf_op args[2]
  11.9 9.8 %states.1 = (bf16[8,10,128,128]{3,2,1,0:T(8,128)(2,1)}, f32[8,10,128]{2,1,0:T(8,128)}, bf16[10,128,128]{2,1,0:T(8,128)(2,1)}, f32[10,128]{1,0:T(8,128)}) custom-call(bf16[1024,1280]{1,0:T(8,128)(2,1)} %x_ref.3, bf16[1024,20]{1,0:T(8,128)(2,1)} %copy.12.raw_ref, f32[1,20]{1,0:T(1,128)} %multiply_bitcast_fusion.rate_ref, ...), custom_call_target="tpu_custom_call" | custom-call | tf_op jit(solution)/shard_map/states/pallas_call | solution.py:229
  21.7 21.4 %exchange.1.coming_ref = f32[10,128,128]{2,1,0:T(8,128)} custom-call(bf16[10,128,128]{2,1,0:T(8,128)(2,1)} %get-tuple-element.13.fin_ref, f32[10,128]{1,0:T(8,128)} %get-tuple-element.14.tot_ref), custom_call_target="tpu_custom_call" | custom-call | tf_op jit(solution)/shard_map/exchange/pallas_call | solution.py:247
  43.1 0.0 copy-done
  43.1 0.1 dynamic_slice.10
  43.2 0.1 broadcast_in_dim.11
  43.3 0.1 broadcast_in_dim.12
  43.3 0.7 broadcast_in_dim.13.skip_ref
  44.0 13.6 %outputs.1 = (bf16[1024,1280]{1,0:T(8,128)(2,1)}, f32[8,1,128]{2,1,0:T(1,128)}) custom-call(bf16[1024,1280]{1,0:T(8,128)(2,1)} %x_ref.3, bf16[1024,1280]{1,0:T(8,128)(2,1)} %z_ref.1, bf16[1024,20]{1,0:T(8,128)(2,1)} %copy.12.raw_ref, f32[1,20]{1,0:T(1,128)} %multiply_bitcast_fusion.rate_ref, bf16[1024,256]{1,0:T(8,128)(2,1)} %all_gather.3.write_ref.read_ref, ...), custom_call_target="tpu_custom_call" | custom-call | tf_op jit(solution)/shard_map/outputs/pallas_call | solution.py:260
  57.6 7.4 %psum.7 = f32[8,1,128]{2,1,0:T(1,128)S(1)} all-reduce(f32[8,1,128]{2,1,0:T(1,128)} %get-tuple-element.16), channel_id=1, replica_groups=mesh['seq'=8,'head'=4] {'head'}, use_global_device_ids=true, to_apply=%region_0.0 | all-reduce | flops 1024 | bytes 8192 | tf_op jit(solution)/shard_map/psum | solution.py:273
  65.1 0.8 %dynamic_slice.11 = f32[1280]{0:T(1024)S(1)} dynamic-slice(f32[5120]{0:T(1024)} %param.15, s32[]{:T(128)S(6)} %select_n.8), dynamic_slice_sizes={1280} | dynamic-slice | bytes 10244 | tf_op jit(solution)/shard_map/dynamic_slice | solution.py:213
  65.9 3.9 %multiply_convert_fusion = bf16[1024,1280]{1,0:T(8,128)(2,1)} fusion(bf16[1024,1280]{1,0:T(8,128)(2,1)} %get-tuple-element.15, f32[1280]{0:T(1024)S(1)} %dynamic_slice.11, f32[1024]{0:T(1024)S(1)} %bitcast.3), kind=kLoop, calls=%fused_computation | loop fusion | flops 5242880 | bytes 5252096 | tf_op jit(solution)/shard_map/convert_element_type | solution.py:275
  (1 shorter events, 0.0 us)
Async XLA Ops:
  2.1 41.0 %copy-start = (f32[80]{0:T(128)S(1)}, f32[80]{0:T(128)}, u32[]{:S(2)}) copy-start(f32[80]{0:T(128)} %param.14) | copy-start | bytes 964

commit v2 on v0

v2 whole, which is shorter than its diff:
```python
import functools
import math

import jax
import jax.numpy as jnp
from jax import lax
from jax.experimental import pallas as pl
from jax.experimental.pallas import tpu as pltpu
from jax.sharding import PartitionSpec as P

HEAD_DIM = 64
L = 128
SLOT = 32
LOG2E = math.log2(math.e)
F32 = jnp.float32
BF16 = jnp.bfloat16
MESH = pl.DeviceIdType.MESH
CAP = 100.0


def pair_lanes(first, second, rows):
    lane = lax.broadcasted_iota(jnp.int32, (rows, L), 1)
    first = jnp.broadcast_to(first, (rows, L))
    second = jnp.broadcast_to(second, (rows, L))
    return jnp.where(lane < HEAD_DIM, first, second)


def layer_kernel(
    count, peers, heads, tiles, group, chunks,
    x_hbm, z_hbm, raw_ref, decay_ref, write_ref, read_ref, skip_ref, gain_ref,
    gated_ref, square_ref,
    x_ref, z_ref, writes, reads, sums, run_rows, cols, masked, local,
    loc, pre, fin, carry, tot, mate_buf, mate_tot, chain_in, chain_out, coming_ref,
    spot, sq, sq_own, sq_in,
    x_sem, z_sem, s_w, r_w, s_r, r_r, s_mate, r_mate, s_tot, r_tot, s_chain, r_chain, s_sq, r_sq,
):
    me = lax.axis_index("seq")
    head = lax.axis_index("head")
    odd = lax.rem(me, 2)
    is_odd = odd == 1
    pairs = count // 2
    place = me // 2
    mate = me + 1 - 2 * odd
    after = lax.rem(me + 2, count)
    before = lax.rem(me + count - 2, count)
    has_before = place > 0
    has_after = place < pairs - 1
    pieces = tiles // group
    width = group * L
    rows = write_ref.shape[0]

    def load_x(p):
        span = pl.ds(p * width, width)
        return pltpu.make_async_copy(x_hbm.at[:, span], x_ref.at[:, span], x_sem.at[p])

    load_z = pltpu.make_async_copy(z_hbm, z_ref, z_sem)
    for p in range(pieces):
        load_x(p).start()
    load_z.start()

    barrier = pltpu.get_barrier_semaphore()
    for other in (mate, after, before):
        pl.semaphore_signal(barrier, inc=1, device_id={"seq": other}, device_id_type=MESH)
    for d in range(1, peers):
        pl.semaphore_signal(
            barrier, inc=1, device_id={"head": lax.rem(head + d, peers)}, device_id_type=MESH
        )
    pl.semaphore_wait(barrier, 3 + peers - 1)

    def to_peer(src, dst, send, recv, d):
        return pltpu.make_async_remote_copy(
            src_ref=src, dst_ref=dst, send_sem=send.at[d - 1], recv_sem=recv.at[d - 1],
            device_id={"head": lax.rem(head + d, peers)}, device_id_type=MESH,
        )

    own_rows = pl.ds(pl.multiple_of(head * rows, L), rows)
    give_w = [to_peer(write_ref, writes.at[own_rows], s_w, r_w, d) for d in range(1, peers)]
    give_r = [to_peer(read_ref, reads.at[own_rows], s_r, r_r, d) for d in range(1, peers)]
    for copy in give_w + give_r:
        copy.start()
    writes[own_rows, :] = write_ref[...]
    reads[own_rows, :] = read_ref[...]

    total_heads = decay_ref.shape[1]
    spot[...] = jnp.zeros_like(spot)
    spot[0:1, :total_heads] = decay_ref[...]
    spot[1:2, :total_heads] = skip_ref[...]
    rolled = pltpu.roll(spot[...], lax.rem(L - head * heads, L), 1)
    skip_row = rolled[1:2, :]
    square = jnp.broadcast_to(rolled[0:1, :], (L, L)).T
    rate = jnp.exp(square[:heads, :1]) * LOG2E
    raw = raw_ref[...].astype(F32)
    step = jnp.maximum(raw, 0.0) + jnp.log1p(jnp.exp(-jnp.abs(raw)))
    falls = -rate * step
    steps = jnp.log2(step)
    sums[...] = jnp.zeros_like(sums)
    for c in range(chunks):
        sums[c, :heads, :] = falls[:, c * L : (c + 1) * L]
    row = lax.broadcasted_iota(jnp.int32, (L, L), 0)
    col = lax.broadcasted_iota(jnp.int32, (L, L), 1)
    upper = jnp.where(row <= col, 1.0, 0.0).astype(F32)
    run_all = jnp.dot(
        sums[...].reshape(chunks * SLOT, L), upper,
        preferred_element_type=F32, precision=lax.Precision.HIGHEST,
    ).reshape(chunks, SLOT, L)
    sums[:, :, :] = jnp.zeros_like(sums)
    for c in range(chunks):
        sums[c, :heads, :] = steps[:, c * L : (c + 1) * L]
    tot[...] = jnp.zeros_like(tot)
    for c in range(chunks):
        run = run_all[c]
        run_u = run - sums[c]
        run_rows[c] = run_u
        last = jnp.broadcast_to(run[:, L - 1 : L], (SLOT, L))
        cols[c] = jnp.concatenate(
            [run, jnp.exp2(run), jnp.exp2(last - run_u), last], axis=0
        ).T
        pre[c] = tot[...]
        for j in range(tiles):
            at = 3 * SLOT + 2 * j
            gone = pair_lanes(cols[c, 0:1, at : at + 1], cols[c, 0:1, at + 1 : at + 2], 1)
            tot[j : j + 1, :] = tot[j : j + 1, :] + gone

    tot_copy = pltpu.make_async_remote_copy(
        src_ref=tot, dst_ref=mate_tot, send_sem=s_tot, recv_sem=r_tot,
        device_id={"seq": mate}, device_id_type=MESH,
    )
    tot_copy.start()
    for copy in give_w:
        copy.wait_recv()

    def to_mate(p):
        part = pl.ds(p * group, group)
        return pltpu.make_async_remote_copy(
            src_ref=fin.at[part], dst_ref=mate_buf.at[part],
            send_sem=s_mate.at[p], recv_sem=r_mate.at[p],
            device_id={"seq": mate}, device_id_type=MESH,
        )

    def to_next(p):
        part = pl.ds(p * group, group)
        return pltpu.make_async_remote_copy(
            src_ref=chain_out.at[part], dst_ref=chain_in.at[part],
            send_sem=s_chain.at[p], recv_sem=r_chain.at[p],
            device_id={"seq": after}, device_id_type=MESH,
        )

    def at_chunk(c):
        return pl.ds(pl.multiple_of(c * L, L), L)

    for p in range(pieces):
        load_x(p).wait()
        carry[...] = jnp.zeros_like(carry)

        def advance(c, _, p=p):
            here = at_chunk(c)
            tail = cols[c]
            weighted = []
            for j in range(p * group, (p + 1) * group):
                at = 2 * SLOT + 2 * j
                wide = pair_lanes(tail[:, at : at + 1], tail[:, at + 1 : at + 2], L)
                x = x_ref[here, j * L : (j + 1) * L].astype(F32)
                weighted.append((wide * x).astype(BF16))
            new = lax.dot_general(
                writes[here, :], jnp.concatenate(weighted, axis=1),
                (((0,), (0,)), ((), ())), preferred_element_type=F32,
            )
            for i in range(group):
                j = p * group + i
                at = 3 * SLOT + 2 * j
                gone = pair_lanes(tail[0:1, at : at + 1], tail[0:1, at + 1 : at + 2], 1)
                old = carry[i]
                loc[c, j] = old.astype(BF16)
                carry[i] = jnp.exp2(gone) * old + new[:, i * L : (i + 1) * L]
            return 0

        lax.fori_loop(0, chunks, advance, 0, unroll=2)
        for i in range(group):
            fin[p * group + i] = carry[i].astype(BF16)
        to_mate(p).start()

    @pl.when(jnp.logical_not(has_before))
    def _():
        chain_in[...] = jnp.zeros_like(chain_in)

    for copy in give_r:
        copy.wait_recv()

    def score(c, _):
        here = at_chunk(c)
        scores = lax.dot_general(
            reads[here, :], writes[here, :], (((1,), (1,)), ((), ())),
            preferred_element_type=F32,
        )
        masked[c] = jnp.where(col <= row, scores, 0.0)
        return 0

    lax.fori_loop(0, chunks, score, 0)
    tot_copy.wait_recv()

    def chain_step(p):
        to_mate(p).wait_recv()

        @pl.when(has_before)
        def _():
            to_next(p).wait_recv()

        for i in range(group):
            j = p * group + i
            own_tot = jnp.exp2(tot[pl.ds(j, 1), :])
            other_tot = jnp.exp2(mate_tot[pl.ds(j, 1), :])
            own = fin[j].astype(F32)
            other = mate_buf[j].astype(F32)
            coming = chain_in[j].astype(F32)
            early = jnp.where(is_odd, other, own)
            late = jnp.where(is_odd, own, other)
            early_tot = jnp.where(is_odd, other_tot, own_tot)
            late_tot = jnp.where(is_odd, own_tot, other_tot)
            middle = early_tot * coming + early
            chain_out[j] = (late_tot * middle + late).astype(BF16)
            coming_ref[j] = jnp.where(is_odd, middle, coming)

        @pl.when(has_after)
        def _():
            to_next(p).start()

    shift = jnp.minimum(place, pieces)
    left = col < HEAD_DIM
    for k in range(pieces):
        due = k - shift

        @pl.when(due >= 0)
        def _():
            chain_step(due)

        def inside(c, _, p=k):
            here = at_chunk(c)
            run = cols[c]
            scores = masked[c]
            for j in range(p * group, (p + 1) * group):
                x = x_ref[here, j * L : (j + 1) * L].astype(F32)
                mixes = []
                for h in (2 * j, 2 * j + 1):
                    spread = run[:, h : h + 1] - run_rows[c, h : h + 1, :]
                    mixes.append((scores * jnp.exp2(jnp.minimum(spread, CAP))).astype(BF16))
                top = jnp.where(left, x, 0.0).astype(BF16)
                bottom = jnp.where(left, 0.0, x).astype(BF16)
                skip = pair_lanes(
                    skip_row[:, 2 * j : 2 * j + 1], skip_row[:, 2 * j + 1 : 2 * j + 2], 1
                )
                local[here, j * L : (j + 1) * L] = skip * x + jnp.dot(
                    jnp.concatenate(mixes, axis=1), jnp.concatenate([top, bottom], axis=0),
                    preferred_element_type=F32,
                )
            return 0

        lax.fori_loop(0, chunks, inside, 0)

    load_z.wait()
    sq[...] = jnp.zeros_like(sq)
    first_gain = pl.multiple_of(head * (tiles * L), L)
    for k in range(pieces):

        @pl.when(k >= pieces - shift)
        def _():
            chain_step(jnp.int32(k))

        gain = gain_ref[:, pl.ds(first_gain + k * width, width)]

        def finish(c, _, p=k, gain=gain):
            here = at_chunk(c)
            grown = cols[c]
            entering = []
            for j in range(p * group, (p + 1) * group):
                entering.append(
                    (
                        loc[c, j].astype(F32) + jnp.exp2(pre[c, j : j + 1, :]) * coming_ref[j]
                    ).astype(BF16)
                )
            inter = jnp.dot(
                reads[here, :], jnp.concatenate(entering, axis=1), preferred_element_type=F32
            )
            squares = sq[c]
            for i in range(group):
                j = p * group + i
                at = SLOT + 2 * j
                span = slice(j * L, (j + 1) * L)
                y = local[here, span] + (
                    pair_lanes(grown[:, at : at + 1], grown[:, at + 1 : at + 2], L)
                    * inter[:, i * L : (i + 1) * L]
                )
                z = z_ref[here, span].astype(F32)
                gated = y * z * jax.nn.sigmoid(z)
                squares = squares + gated * gated
                gated_ref[here, span] = (gated * gain[:, i * L : (i + 1) * L]).astype(BF16)
            sq[c] = squares
            return 0

        lax.fori_loop(0, chunks, finish, 0)

    for c in range(chunks):
        sq_own[c : c + 1, :] = jnp.sum(sq[c].T, axis=0, keepdims=True)
    give_sq = [to_peer(sq_own, sq_in.at[d - 1], s_sq, r_sq, d) for d in range(1, peers)]
    for copy in give_sq:
        copy.start()
    square_sum = sq_own[...]
    for d in range(1, peers):
        give_sq[d - 1].wait_recv()
        square_sum = square_sum + sq_in[d - 1]
    square_ref[...] = square_sum

    tot_copy.wait_send()
    for copy in give_w + give_r + give_sq:
        copy.wait_send()
    for p in range(pieces):
        to_mate(p).wait_send()

        @pl.when(has_after)
        def _():
            to_next(p).wait_send()


def scale_kernel(part, channels, gated_ref, square_ref, out_ref):
    i = pl.program_id(0)
    for k in range(part):
        sums = square_ref[pl.ds(i * part + k, 1), :]
        factor = lax.rsqrt(jnp.broadcast_to(sums, (L, L)).T / channels + 1e-05)
        here = slice(k * L, (k + 1) * L)
        for j in range(gated_ref.shape[1] // L):
            span = slice(j * L, (j + 1) * L)
            out_ref[here, span] = (gated_ref[here, span].astype(F32) * factor).astype(BF16)


def on_device(
    count, peers, head_inputs, gate_inputs, step_raw, decay_log, state_write, state_read, skip_gain, norm_gain
):
    tokens, inner = head_inputs.shape
    heads = inner // HEAD_DIM
    tiles = inner // L
    chunks = tokens // L
    states = state_write.shape[1]
    group = math.gcd(tiles, 2)
    pieces = tiles // group
    sds = jax.ShapeDtypeStruct
    vmem = pl.BlockSpec(memory_space=pltpu.VMEM)
    hbm = pl.BlockSpec(memory_space=pl.ANY)
    dma = pltpu.SemaphoreType.DMA
    state = (tiles, states, L)
    gated, squares = pl.pallas_call(
        functools.partial(layer_kernel, count, peers, heads, tiles, group, chunks),
        in_specs=[hbm, hbm] + [vmem] * 6,
        out_specs=[vmem, vmem],
        out_shape=[sds((tokens, inner), BF16), sds((chunks, L), F32)],
        scratch_shapes=[
            pltpu.VMEM((tokens, inner), BF16),
            pltpu.VMEM((tokens, inner), BF16),
            pltpu.VMEM((tokens, states), BF16),
            pltpu.VMEM((tokens, states), BF16),
            pltpu.VMEM((chunks, SLOT, L), F32),
            pltpu.VMEM((chunks, SLOT, L), F32),
            pltpu.VMEM((chunks, L, L), F32),
            pltpu.VMEM((chunks, L, L), F32),
            pltpu.VMEM((tokens, inner), F32),
            pltpu.VMEM((chunks,) + state, BF16),
            pltpu.VMEM((chunks, tiles, L), F32),
            pltpu.VMEM(state, BF16),
            pltpu.VMEM((group, states, L), F32),
            pltpu.VMEM((tiles, L), F32),
            pltpu.VMEM(state, BF16),
            pltpu.VMEM((tiles, L), F32),
            pltpu.VMEM(state, BF16),
            pltpu.VMEM(state, BF16),
            pltpu.VMEM(state, F32),
            pltpu.VMEM((8, L), F32),
            pltpu.VMEM((chunks, L, L), F32),
            pltpu.VMEM((chunks, L), F32),
            pltpu.VMEM((peers - 1, chunks, L), F32),
            dma((pieces,)), dma,
            dma((peers - 1,)), dma((peers - 1,)), dma((peers - 1,)), dma((peers - 1,)),
            dma((pieces,)), dma((pieces,)), dma, dma, dma((pieces,)), dma((pieces,)),
            dma((peers - 1,)), dma((peers - 1,)),
        ],
        compiler_params=pltpu.CompilerParams(
            collective_id=0, has_side_effects=True, vmem_limit_bytes=50 * 2**20
        ),
        name="layer",
    )(
        head_inputs, gate_inputs, step_raw.T, decay_log.reshape(1, -1),
        state_write, state_read, skip_gain.reshape(1, -1), norm_gain.reshape(1, -1),
    )
    part = 2
    wide = pl.BlockSpec((part * L, inner), lambda c: (c, 0))
    return pl.pallas_call(
        functools.partial(scale_kernel, part, norm_gain.shape[0]),
        grid=(chunks // part,),
        in_specs=[wide, pl.BlockSpec((chunks, L), lambda c: (0, 0))],
        out_specs=wide,
        out_shape=sds((tokens, inner), BF16),
        name="scale",
    )(gated, squares)


def solution(mesh):
    return jax.shard_map(
        functools.partial(on_device, mesh.shape["seq"], mesh.shape["head"]),
        mesh=mesh,
        in_specs=(
            P("seq", "head"),
            P("seq", "head"),
            P("seq", "head"),
            P(),
            P(("seq", "head"), None),
            P(("seq", "head"), None),
            P(),
            P(),
        ),
        out_specs=P("seq", "head"),
        check_vma=False,
    )
```

time: 175 us -> 58.6 us (0.33); the launches traced: 172 us -> 58.2 us
  Pallas kernels: 0 us -> 51.6 us
  local copies, waits for them, and re-layouts: 54.4 us -> 6.61 us
  blocking collectives: 33.6 us -> 0 us
  other arithmetic: 27.1 us -> 0 us
  waiting for transfers between devices: 22.4 us -> 0 us
  matrix products: 19.9 us -> 0 us
  between operations: 14.3 us -> 0.02 us
    pallas_call x0 -> x2, Pallas kernels: none -> 51.6 us  [the longest x1 47.3 us: on_device(): pl.pallas_call(functools.partial(layer_kernel, count, peers, heads, tiles...]
    all_gather x1 -> x0, waiting for transfers between devices: 22.4 us -> none  [entering_2(): gathered = jax.tree.map(lambda a: lax.all_gather(a, axis), part)]
    dot_general x8 -> x0, matrix products: 19.9 us -> none  [the longest x5 12.2 us: intra_block(): jnp.einsum('khtu,kuhp->kthp', mixing, values, preferred_element_type=jnp....]
    convert_element_type x3 -> x0, local copies, waits for them, and re-layouts: 17.1 us -> none  [the longest x2 12.7 us: block_pieces(): local = local + skip_gain[:, None] * shaped.astype(jnp.float32)]
    unnamed x1 -> x0, blocking collectives: 15.6 us -> none
    all_gather x2 -> x0, blocking collectives: 12.3 us -> none  [the longest x1 6.5 us: on_device(): lax.all_gather(state_write, 'head', axis=0, tiled=True)]
    dynamic_slice x22 -> x0, local copies, waits for them, and re-layouts: 11.2 us -> none  [the longest x20 9.83 us: block_pieces(): mixed_groups = lax.map(per_group, (split_values, split_running, split_step))]
    convert_element_type x2 -> x0, other arithmetic: 8.66 us -> none  [the longest x1 4.97 us: on_device(): return (gated * factor * gains).astype(jnp.bfloat16)]
  transfers between devices with their start and end apart: 1 -> 0, of which waited for: 1 -> 0; matrix products, arithmetic and copies ran while one was open for 24% -> 0% of each run, Pallas kernels for 0% -> 0%
where the time goes in v2:
time: 58.6 us; the launch traced here: 58.2 us
  Pallas kernels  51.6 us (88%)
  local copies, waits for them, and re-layouts  6.61 us (11%)
    pallas_call x1, Pallas kernels, on_device(): pl.pallas_call(functools.partial(layer_kernel, count, peers, heads, tiles...  47.3 us
    unnamed x16, local copies, waits for them, and re-layouts  6.61 us
    pallas_call x1, Pallas kernels, on_device(): pl.pallas_call(functools.partial(scale_kernel, part, norm_gain.shape[0]),...  4.33 us

profile of v2, /device:TPU:25, one launch (start us, length us, event | category | flops | bytes accessed | tf_op | source)
XLA Modules:
  0.0 58.2 jit_solution(6347199700780086985)
XLA Ops:
  0.0 0.0 copy-start.1
  0.0 0.8 %copy-done.1 = bf16[256,128]{1,0:T(8,128)(2,1)S(1)} copy-done((bf16[256,128]{1,0:T(8,128)(2,1)S(1)}, bf16[256,128]{1,0:T(8,128)(2,1)}, u32[]{:S(2)}) %copy-start.1) | copy-done | bytes 65560
  0.8 0.0 copy-start.2
  0.8 0.8 %copy-done.2 = bf16[256,128]{1,0:T(8,128)(2,1)S(1)} copy-done((bf16[256,128]{1,0:T(8,128)(2,1)S(1)}, bf16[256,128]{1,0:T(8,128)(2,1)}, u32[]{:S(2)}) %copy-start.2) | copy-done | bytes 65560
  1.7 0.0 copy-start.3
  1.7 0.8 %copy-done.3 = bf16[1024,20]{0,1:T(8,128)(2,1)S(1)} copy-done((bf16[1024,20]{0,1:T(8,128)(2,1)S(1)}, bf16[1024,20]{0,1:T(8,128)(2,1)}, u32[]{:S(2)}) %copy-start.3) | copy-done | bytes 40984
  2.5 0.0 copy-start.4
  2.5 0.7 %copy-done.4 = f32[5120]{0:T(1024)S(1)} copy-done((f32[5120]{0:T(1024)S(1)}, f32[5120]{0:T(1024)}, u32[]{:S(2)}) %copy-start.4) | copy-done | bytes 20504
  3.2 0.0 copy-start.6
  3.2 0.7 %copy-done.6 = f32[80]{0:T(128)S(1)} copy-done((f32[80]{0:T(128)S(1)}, f32[80]{0:T(128)}, u32[]{:S(2)}) %copy-start.6) | copy-done | bytes 344
  3.9 0.0 copy-start.7
  3.9 0.7 %copy-done.7 = f32[80]{0:T(128)S(1)} copy-done((f32[80]{0:T(128)S(1)}, f32[80]{0:T(128)}, u32[]{:S(2)}) %copy-start.7) | copy-done | bytes 344
  4.5 47.3 %layer.1 = (bf16[1024,1280]{1,0:T(8,128)(2,1)S(1)}, f32[8,128]{1,0:T(8,128)S(1)}) custom-call(bf16[1024,1280]{1,0:T(8,128)(2,1)} %x_hbm.1, bf16[1024,1280]{1,0:T(8,128)(2,1)} %z_hbm.1, bf16[20,1024]{1,0:T(8,128)(2,1)S(1)} %bitcast.4, f32[1,80]{1,0:T(1,128)S(1)} %bitcast.6, bf16[256,128]{1,0:T(8,128)(2,1)S(1)} %copy-done.1, bf16[256,128]{1,0:T(8,128)(2,1)S(1)} %copy-done.2, ...), custom_call_target="tpu_custom_call" | custom-call | tf_op jit(solution)/shard_map/layer/pallas_call | solution.py:349
  51.8 0.0 copy-start
  51.8 1.5 %copy-done = bf16[1024,1280]{1,0:T(8,128)(2,1)} copy-done((bf16[1024,1280]{1,0:T(8,128)(2,1)}, bf16[1024,1280]{1,0:T(8,128)(2,1)S(1)}, u32[]{:S(2)}) %copy-start) | copy-done | bytes 2621464
  53.3 0.0 copy-start.5
  53.3 0.6 %copy-done.5 = f32[8,128]{1,0:T(8,128)} copy-done((f32[8,128]{1,0:T(8,128)}, f32[8,128]{1,0:T(8,128)S(1)}, u32[]{:S(2)}) %copy-start.5) | copy-done | bytes 4120
  53.9 4.3 %scale.1 = bf16[1024,1280]{1,0:T(8,128)(2,1)} custom-call(bf16[1024,1280]{1,0:T(8,128)(2,1)} %copy-done, f32[8,128]{1,0:T(8,128)} %copy-done.5), custom_call_target="tpu_custom_call" | custom-call | tf_op jit(solution)/shard_map/scale/pallas_call | solution.py:393
Async XLA Ops:
  0.0 0.8 %copy-start.1 = (bf16[256,128]{1,0:T(8,128)(2,1)S(1)}, bf16[256,128]{1,0:T(8,128)(2,1)}, u32[]{:S(2)}) copy-start(bf16[256,128]{1,0:T(8,128)(2,1)} %write_ref.1) | copy-start | bytes 196612
  0.8 0.8 %copy-start.2 = (bf16[256,128]{1,0:T(8,128)(2,1)S(1)}, bf16[256,128]{1,0:T(8,128)(2,1)}, u32[]{:S(2)}) copy-start(bf16[256,128]{1,0:T(8,128)(2,1)} %read_ref.1) | copy-start | bytes 196612
  1.7 0.8 %copy-start.3 = (bf16[1024,20]{0,1:T(8,128)(2,1)S(1)}, bf16[1024,20]{0,1:T(8,128)(2,1)}, u32[]{:S(2)}) copy-start(bf16[1024,20]{0,1:T(8,128)(2,1)} %param.10) | copy-start | bytes 122884
  2.5 0.7 %copy-start.4 = (f32[5120]{0:T(1024)S(1)}, f32[5120]{0:T(1024)}, u32[]{:S(2)}) copy-start(f32[5120]{0:T(1024)} %param.15) | copy-start | bytes 61444
  3.2 0.7 %copy-start.6 = (f32[80]{0:T(128)S(1)}, f32[80]{0:T(128)}, u32[]{:S(2)}) copy-start(f32[80]{0:T(128)} %param.11) | copy-start | bytes 964
  3.9 0.7 %copy-start.7 = (f32[80]{0:T(128)S(1)}, f32[80]{0:T(128)}, u32[]{:S(2)}) copy-start(f32[80]{0:T(128)} %param.14) | copy-start | bytes 964
  51.8 1.5 %copy-start = (bf16[1024,1280]{1,0:T(8,128)(2,1)}, bf16[1024,1280]{1,0:T(8,128)(2,1)S(1)}, u32[]{:S(2)}) copy-start(bf16[1024,1280]{1,0:T(8,128)(2,1)S(1)} %get-tuple-element.7.gated_ref) | copy-start | bytes 7864324
  53.3 0.6 %copy-start.5 = (f32[8,128]{1,0:T(8,128)}, f32[8,128]{1,0:T(8,128)S(1)}, u32[]{:S(2)}) copy-start(f32[8,128]{1,0:T(8,128)S(1)} %get-tuple-element.8.square_ref) | copy-start | bytes 12292

commit v3 on v2

--- a/solution.py
+++ b/solution.py
@@ -16,6 +16,9 @@
 BF16 = jnp.bfloat16
 MESH = pl.DeviceIdType.MESH
 CAP = 100.0
+UNROLL = 4
+LEAD = 3
+HOP = 2
 
 
 def pair_lanes(first, second, rows):
@@ -27,12 +30,12 @@
 
 def layer_kernel(
     count, peers, heads, tiles, group, chunks,
-    x_hbm, z_hbm, raw_ref, decay_ref, write_ref, read_ref, skip_ref, gain_ref,
-    gated_ref, square_ref,
+    x_hbm, z_hbm, raw_hbm, decay_hbm, write_hbm, read_hbm, skip_hbm, gain_hbm,
+    gated_hbm, square_ref, gated_ref, out_sem, raw_ref, decay_ref, skip_ref, gain_ref, writes_t,
     x_ref, z_ref, writes, reads, sums, run_rows, cols, masked, local,
     loc, pre, fin, carry, tot, mate_buf, mate_tot, chain_in, chain_out, coming_ref,
     spot, sq, sq_own, sq_in,
-    x_sem, z_sem, s_w, r_w, s_r, r_r, s_mate, r_mate, s_tot, r_tot, s_chain, r_chain, s_sq, r_sq,
+    x_sem, z_sem, in_sem, s_w, r_w, s_r, r_r, s_mate, r_mate, s_tot, r_tot, s_chain, r_chain, s_sq, r_sq,
 ):
     me = lax.axis_index("seq")
     head = lax.axis_index("head")
@@ -47,11 +50,33 @@
     has_after = place < pairs - 1
     pieces = tiles // group
     width = group * L
-    rows = write_ref.shape[0]
+    rows = write_hbm.shape[0]
+    own_rows = pl.ds(pl.multiple_of(head * rows, L), rows)
+    inputs = [
+        pltpu.make_async_copy(source, target, in_sem.at[i])
+        for i, (source, target) in enumerate(
+            [
+                (write_hbm, writes.at[own_rows]),
+                (read_hbm, reads.at[own_rows]),
+                (raw_hbm, raw_ref),
+                (decay_hbm, decay_ref),
+                (skip_hbm, skip_ref),
+                (gain_hbm, gain_ref),
+            ]
+        )
+    ]
+    for copy in inputs:
+        copy.start()
 
     def load_x(p):
         span = pl.ds(p * width, width)
         return pltpu.make_async_copy(x_hbm.at[:, span], x_ref.at[:, span], x_sem.at[p])
+
+    def store(p):
+        span = pl.ds(p * width, width)
+        return pltpu.make_async_copy(
+            gated_ref.at[:, span], gated_hbm.at[:, span], out_sem.at[p]
+        )
 
     load_z = pltpu.make_async_copy(z_hbm, z_ref, z_sem)
     for p in range(pieces):
@@ -73,13 +98,16 @@
             device_id={"head": lax.rem(head + d, peers)}, device_id_type=MESH,
         )
 
-    own_rows = pl.ds(pl.multiple_of(head * rows, L), rows)
-    give_w = [to_peer(write_ref, writes.at[own_rows], s_w, r_w, d) for d in range(1, peers)]
-    give_r = [to_peer(read_ref, reads.at[own_rows], s_r, r_r, d) for d in range(1, peers)]
-    for copy in give_w + give_r:
+    give_w = [to_peer(writes.at[own_rows], writes.at[own_rows], s_w, r_w, d) for d in range(1, peers)]
+    give_r = [to_peer(reads.at[own_rows], reads.at[own_rows], s_r, r_r, d) for d in range(1, peers)]
+    inputs[0].wait()
+    for copy in give_w:
         copy.start()
-    writes[own_rows, :] = write_ref[...]
-    reads[own_rows, :] = read_ref[...]
+    inputs[1].wait()
+    for copy in give_r:
+        copy.start()
+    for copy in inputs[2:]:
+        copy.wait()
 
     total_heads = decay_ref.shape[1]
     spot[...] = jnp.zeros_like(spot)
@@ -128,6 +156,8 @@
     tot_copy.start()
     for copy in give_w:
         copy.wait_recv()
+    for c in range(chunks):
+        writes_t[c] = writes[c * L : (c + 1) * L, :].astype(F32).T.astype(BF16)
 
     def to_mate(p):
         part = pl.ds(p * group, group)
@@ -147,56 +177,6 @@
 
     def at_chunk(c):
         return pl.ds(pl.multiple_of(c * L, L), L)
-
-    for p in range(pieces):
-        load_x(p).wait()
-        carry[...] = jnp.zeros_like(carry)
-
-        def advance(c, _, p=p):
-            here = at_chunk(c)
-            tail = cols[c]
-            weighted = []
-            for j in range(p * group, (p + 1) * group):
-                at = 2 * SLOT + 2 * j
-                wide = pair_lanes(tail[:, at : at + 1], tail[:, at + 1 : at + 2], L)
-                x = x_ref[here, j * L : (j + 1) * L].astype(F32)
-                weighted.append((wide * x).astype(BF16))
-            new = lax.dot_general(
-                writes[here, :], jnp.concatenate(weighted, axis=1),
-                (((0,), (0,)), ((), ())), preferred_element_type=F32,
-            )
-            for i in range(group):
-                j = p * group + i
-                at = 3 * SLOT + 2 * j
-                gone = pair_lanes(tail[0:1, at : at + 1], tail[0:1, at + 1 : at + 2], 1)
-                old = carry[i]
-                loc[c, j] = old.astype(BF16)
-                carry[i] = jnp.exp2(gone) * old + new[:, i * L : (i + 1) * L]
-            return 0
-
-        lax.fori_loop(0, chunks, advance, 0, unroll=2)
-        for i in range(group):
-            fin[p * group + i] = carry[i].astype(BF16)
-        to_mate(p).start()
-
-    @pl.when(jnp.logical_not(has_before))
-    def _():
-        chain_in[...] = jnp.zeros_like(chain_in)
-
-    for copy in give_r:
-        copy.wait_recv()
-
-    def score(c, _):
-        here = at_chunk(c)
-        scores = lax.dot_general(
-            reads[here, :], writes[here, :], (((1,), (1,)), ((), ())),
-            preferred_element_type=F32,
-        )
-        masked[c] = jnp.where(col <= row, scores, 0.0)
-        return 0
-
-    lax.fori_loop(0, chunks, score, 0)
-    tot_copy.wait_recv()
 
     def chain_step(p):
         to_mate(p).wait_recv()
@@ -224,14 +204,72 @@
         def _():
             to_next(p).start()
 
-    shift = jnp.minimum(place, pieces)
+    def maybe_step(slot):
+        due = slot - shift
+
+        @pl.when(jnp.logical_and(due >= 0, due < pieces))
+        def _():
+            chain_step(due)
+
+    lead = min(LEAD, pieces)
+    shift = jnp.minimum(lead + HOP * place, 2 * pieces)
+
+    @pl.when(jnp.logical_not(has_before))
+    def _():
+        chain_in[...] = jnp.zeros_like(chain_in)
+
+    for p in range(pieces):
+        if p == lead:
+            tot_copy.wait_recv()
+        if p >= lead:
+            maybe_step(p)
+        load_x(p).wait()
+        carry[...] = jnp.zeros_like(carry)
+
+        def advance(c, _, p=p):
+            here = at_chunk(c)
+            tail = cols[c]
+            weighted = []
+            for j in range(p * group, (p + 1) * group):
+                at = 2 * SLOT + 2 * j
+                wide = pair_lanes(tail[:, at : at + 1], tail[:, at + 1 : at + 2], L)
+                x = x_ref[here, j * L : (j + 1) * L].astype(F32)
+                weighted.append((wide * x).astype(BF16))
+            new = jnp.dot(
+                writes_t[c], jnp.concatenate(weighted, axis=1), preferred_element_type=F32
+            )
+            for i in range(group):
+                j = p * group + i
+                at = 3 * SLOT + 2 * j
+                gone = pair_lanes(tail[0:1, at : at + 1], tail[0:1, at + 1 : at + 2], 1)
+                old = carry[i]
+                loc[c, j] = old.astype(BF16)
+                carry[i] = jnp.exp2(gone) * old + new[:, i * L : (i + 1) * L]
+            return 0
+
+        lax.fori_loop(0, chunks, advance, 0, unroll=UNROLL)
+        for i in range(group):
+            fin[p * group + i] = carry[i].astype(BF16)
+        to_mate(p).start()
+
+    if lead >= pieces:
+        tot_copy.wait_recv()
+    for copy in give_r:
+        copy.wait_recv()
+
+    def score(c, _):
+        here = at_chunk(c)
+        scores = lax.dot_general(
+            reads[here, :], writes[here, :], (((1,), (1,)), ((), ())),
+            preferred_element_type=F32,
+        )
+        masked[c] = jnp.where(col <= row, scores, 0.0)
+        return 0
+
+    lax.fori_loop(0, chunks, score, 0, unroll=UNROLL)
     left = col < HEAD_DIM
     for k in range(pieces):
-        due = k - shift
-
-        @pl.when(due >= 0)
-        def _():
-            chain_step(due)
+        maybe_step(pieces + k)
 
         def inside(c, _, p=k):
             here = at_chunk(c)
@@ -254,14 +292,14 @@
                 )
             return 0
 
-        lax.fori_loop(0, chunks, inside, 0)
+        lax.fori_loop(0, chunks, inside, 0, unroll=UNROLL)
 
     load_z.wait()
     sq[...] = jnp.zeros_like(sq)
     first_gain = pl.multiple_of(head * (tiles * L), L)
     for k in range(pieces):
 
-        @pl.when(k >= pieces - shift)
+        @pl.when(k + shift >= 2 * pieces)
         def _():
             chain_step(jnp.int32(k))
 
@@ -296,7 +334,8 @@
             sq[c] = squares
             return 0
 
-        lax.fori_loop(0, chunks, finish, 0)
+        lax.fori_loop(0, chunks, finish, 0, unroll=UNROLL)
+        store(k).start()
 
     for c in range(chunks):
         sq_own[c : c + 1, :] = jnp.sum(sq[c].T, axis=0, keepdims=True)
@@ -313,6 +352,7 @@
     for copy in give_w + give_r + give_sq:
         copy.wait_send()
     for p in range(pieces):
+        store(p).wait()
         to_mate(p).wait_send()
 
         @pl.when(has_after)
@@ -343,15 +383,22 @@
     pieces = tiles // group
     sds = jax.ShapeDtypeStruct
     vmem = pl.BlockSpec(memory_space=pltpu.VMEM)
-    hbm = pl.BlockSpec(memory_space=pl.ANY)
+    hbm = pl.BlockSpec(memory_space=pltpu.HBM)
     dma = pltpu.SemaphoreType.DMA
     state = (tiles, states, L)
     gated, squares = pl.pallas_call(
         functools.partial(layer_kernel, count, peers, heads, tiles, group, chunks),
-        in_specs=[hbm, hbm] + [vmem] * 6,
-        out_specs=[vmem, vmem],
+        in_specs=[hbm] * 8,
+        out_specs=[hbm, vmem],
         out_shape=[sds((tokens, inner), BF16), sds((chunks, L), F32)],
         scratch_shapes=[
+            pltpu.VMEM((tokens, inner), BF16),
+            dma((pieces,)),
+            pltpu.VMEM((heads, tokens), BF16),
+            pltpu.VMEM((1, decay_log.shape[0]), F32),
+            pltpu.VMEM((1, skip_gain.shape[0]), F32),
+            pltpu.VMEM((1, norm_gain.shape[0]), F32),
+            pltpu.VMEM((chunks, states, L), BF16),
             pltpu.VMEM((tokens, inner), BF16),
             pltpu.VMEM((tokens, inner), BF16),
             pltpu.VMEM((tokens, states), BF16),
@@ -375,13 +422,13 @@
             pltpu.VMEM((chunks, L, L), F32),
             pltpu.VMEM((chunks, L), F32),
             pltpu.VMEM((peers - 1, chunks, L), F32),
-            dma((pieces,)), dma,
+            dma((pieces,)), dma, dma((6,)),
             dma((peers - 1,)), dma((peers - 1,)), dma((peers - 1,)), dma((peers - 1,)),
             dma((pieces,)), dma((pieces,)), dma, dma, dma((pieces,)), dma((pieces,)),
             dma((peers - 1,)), dma((peers - 1,)),
         ],
         compiler_params=pltpu.CompilerParams(
-            collective_id=0, has_side_effects=True, vmem_limit_bytes=50 * 2**20
+            collective_id=0, has_side_effects=True, vmem_limit_bytes=67043328
         ),
         name="layer",
     )(

time: 58.6 us -> 40.5 us (0.69)
  Pallas kernels: 51.6 us -> 40.3 us
  local copies, waits for them, and re-layouts: 6.61 us -> 0 us
    pallas_call x1, Pallas kernels: 47.3 us -> 36 us  [on_device(): pl.pallas_call(functools.partial(layer_kernel, count, peers, heads, tiles...]
    unnamed x16 -> x0, local copies, waits for them, and re-layouts: 6.61 us -> none
where the time goes in v3:
time: 40.5 us; the launch traced here: 40.3 us
  Pallas kernels  40.3 us (100%)
    pallas_call x1, Pallas kernels, on_device(): pl.pallas_call(functools.partial(layer_kernel, count, peers, heads, tiles...  36 us
    pallas_call x1, Pallas kernels, on_device(): pl.pallas_call(functools.partial(scale_kernel, part, norm_gain.shape[0]),...  4.34 us

profile of v3, /device:TPU:25, one launch (start us, length us, event | category | flops | bytes accessed | tf_op | source)
XLA Modules:
  0.0 40.3 jit_solution(3712639747275153253)
XLA Ops:
  0.0 36.0 %layer.1 = (bf16[1024,1280]{1,0:T(8,128)(2,1)}, f32[8,128]{1,0:T(8,128)}) custom-call(bf16[1024,1280]{1,0:T(8,128)(2,1)} %x_hbm.1, bf16[1024,1280]{1,0:T(8,128)(2,1)} %z_hbm.1, bf16[20,1024]{1,0:T(8,128)(2,1)} %bitcast.4, f32[1,80]{1,0:T(1,128)} %bitcast.6, bf16[256,128]{1,0:T(8,128)(2,1)} %write_hbm.1, bf16[256,128]{1,0:T(8,128)(2,1)} %read_hbm.1, ...), custom_call_target="tpu_custom_call" | custom-call | tf_op jit(solution)/shard_map/layer/pallas_call | solution.py:389
  36.0 4.3 %scale.1 = bf16[1024,1280]{1,0:T(8,128)(2,1)} custom-call(bf16[1024,1280]{1,0:T(8,128)(2,1)} %get-tuple-element.7.gated_ref, f32[8,128]{1,0:T(8,128)} %get-tuple-element.8.square_ref), custom_call_target="tpu_custom_call" | custom-call | tf_op jit(solution)/shard_map/scale/pallas_call | solution.py:440

commit v4 on v3

--- a/solution.py
+++ b/solution.py
@@ -18,7 +18,7 @@
 CAP = 100.0
 UNROLL = 4
 LEAD = 3
-HOP = 2
+HOP = 3
 
 
 def pair_lanes(first, second, rows):

time: 40.5 us -> 41.1 us (1.015)
  Pallas kernels: 40.3 us -> 40.9 us
    pallas_call x1, Pallas kernels: 36 us -> 36.6 us  [on_device(): pl.pallas_call(functools.partial(layer_kernel, count, peers, heads, tiles...]
where the time goes in v4:
time: 41.1 us; the launch traced here: 40.9 us
  Pallas kernels  40.9 us (100%)
    pallas_call x1, Pallas kernels, on_device(): pl.pallas_call(functools.partial(layer_kernel, count, peers, heads, tiles...  36.6 us
    pallas_call x1, Pallas kernels, on_device(): pl.pallas_call(functools.partial(scale_kernel, part, norm_gain.shape[0]),...  4.34 us

profile of v4, /device:TPU:25, one launch (start us, length us, event | category | flops | bytes accessed | tf_op | source)
XLA Modules:
  0.0 40.9 jit_solution(17105132739919415195)
XLA Ops:
  0.0 36.6 %layer.1 = (bf16[1024,1280]{1,0:T(8,128)(2,1)}, f32[8,128]{1,0:T(8,128)}) custom-call(bf16[1024,1280]{1,0:T(8,128)(2,1)} %x_hbm.1, bf16[1024,1280]{1,0:T(8,128)(2,1)} %z_hbm.1, bf16[20,1024]{1,0:T(8,128)(2,1)} %bitcast.4, f32[1,80]{1,0:T(1,128)} %bitcast.6, bf16[256,128]{1,0:T(8,128)(2,1)} %write_hbm.1, bf16[256,128]{1,0:T(8,128)(2,1)} %read_hbm.1, ...), custom_call_target="tpu_custom_call" | custom-call | tf_op jit(solution)/shard_map/layer/pallas_call | solution.py:389
  36.6 4.3 %scale.1 = bf16[1024,1280]{1,0:T(8,128)(2,1)} custom-call(bf16[1024,1280]{1,0:T(8,128)(2,1)} %get-tuple-element.7.gated_ref, f32[8,128]{1,0:T(8,128)} %get-tuple-element.8.square_ref), custom_call_target="tpu_custom_call" | custom-call | tf_op jit(solution)/shard_map/scale/pallas_call | solution.py:440
